TPU v7x, 32 devices: a whole 2x2x4 slice. The times are simulated.
32 devices in a mesh: seq: 16 (over z, y, x), head: 2 (over core).
Axes of the slice: x: 2, y: 2, z: 4, core: 2. Of those that a mesh axis runs over, the one named last changes fastest.
Arguments:
- tokens: bfloat16 [16384, 2048], P('seq'), may hold values from -6 to 6
- w_query: bfloat16 [2048, 256], P(None, 'head'), may hold values from -0.25 to 0.25
- w_key: bfloat16 [2048, 256], P(None, 'head'), may hold values from -0.25 to 0.25
- w_value: bfloat16 [2048, 2048], P(None, 'head'), may hold values from -0.125 to 0.125
- w_out: bfloat16 [2048, 2048], replicated, may hold values from -1.796875 to 1.796875
Outputs:
- mixed: bfloat16 [16384, 2048], P('seq', 'head')
All inputs are finite; a program needn't handle non-finite values.
Results may differ from a plain program's by a relative error of at most 0.011.
Values may be sent and summed in bfloat16 or wider, within the bound.
A program may use at most 128 MiB of HBM per device.

v0:
```python
import jax
import jax.numpy as jnp
import numpy as np
from jax import lax
from jax.sharding import PartitionSpec as P

D = 2048
KEY_DIM = 16
VALUE_DIM = 128


def entering(part, axis, combine, identity):
    place = lax.axis_index(axis)
    gathered = jax.tree.map(lambda a: lax.all_gather(a, axis), part)
    state = jax.tree.map(lambda a, e: jnp.zeros_like(a) + jnp.asarray(e, a.dtype), part, identity)

    def one(lap, state):
        return combine(
            state, jax.tree.map(lambda a: lax.dynamic_index_in_dim(a, lap, 0, False), gathered)
        )

    return lax.fori_loop(0, place, one, state)


def taylor_features(rows):
    wide = rows.astype(jnp.float32)
    count = wide.shape[-1]
    outer = (wide[..., :, None] * wide[..., None, :]).reshape(wide.shape[:-1] + (count * count,))
    ones = jnp.ones(wide.shape[:-1] + (1,), jnp.float32)
    joined = jnp.concatenate([ones, wide / count**0.25, outer / (2.0 * count) ** 0.5], axis=-1)
    return joined.astype(jnp.bfloat16)


def packing_tables(count):
    kept_rows = list(range(1 + count))
    mirror_rows = list(range(1 + count))
    off_diagonal = [False] * (1 + count)
    for first in range(count):
        for second in range(first, count):
            kept_rows.append(1 + count + first * count + second)
            mirror_rows.append(1 + count + second * count + first)
            off_diagonal.append(first != second)
    return (np.array(kept_rows, np.int32), np.array(mirror_rows, np.int32), np.array(off_diagonal))


def add_pair(earlier, later):
    return (earlier[0] + later[0], earlier[1] + later[1])


def per_device(tokens, w_query, w_key, w_value, w_out):
    tok_rows = tokens.shape[0]
    heads_here = w_query.shape[1] // KEY_DIM
    queries = (
        jnp.dot(tokens, w_query, preferred_element_type=jnp.float32)
        .astype(jnp.bfloat16)
        .reshape(tok_rows, heads_here, KEY_DIM)
    )
    key_rows = (
        jnp.dot(tokens, w_key, preferred_element_type=jnp.float32)
        .astype(jnp.bfloat16)
        .reshape(tok_rows, heads_here, KEY_DIM)
    )
    val_rows = (
        jnp.dot(tokens, w_value, preferred_element_type=jnp.float32)
        .astype(jnp.bfloat16)
        .reshape(tok_rows, heads_here, VALUE_DIM)
    )
    query_feat = taylor_features(queries)
    key_feat = taylor_features(key_rows)
    state = jnp.einsum("thf,thv->hfv", key_feat, val_rows, preferred_element_type=jnp.float32)
    norm_sum = jnp.sum(key_feat.astype(jnp.float32), axis=0)
    kept_rows, mirror_rows, off_diagonal = packing_tables(KEY_DIM)
    packed_state = state[:, kept_rows] + jnp.where(
        off_diagonal[None, :, None], state[:, mirror_rows], 0.0
    )
    packed_norm = norm_sum[:, kept_rows] + jnp.where(
        off_diagonal[None, :], norm_sum[:, mirror_rows], 0.0
    )
    zero_pair = (jnp.zeros_like(packed_state), jnp.zeros_like(packed_norm))
    prefix, zprefix = entering((packed_state, packed_norm), "seq", add_pair, zero_pair)
    used_feat = query_feat[:, :, kept_rows]
    prefix_low = prefix.astype(jnp.bfloat16)
    numer_pre = jnp.einsum(
        "thf,hfv->thv", used_feat, prefix_low, preferred_element_type=jnp.float32
    )
    denom_pre = jnp.einsum(
        "thf,hf->th", used_feat.astype(jnp.float32), zprefix, precision=lax.Precision.HIGHEST
    )
    block = min(512, tok_rows)
    outputs = []
    for index in range(tok_rows // block):
        low = index * block
        high = low + block
        scores = (
            jnp.einsum(
                "qhd,khd->hqk",
                queries[low:high],
                key_rows[:high],
                preferred_element_type=jnp.float32,
            )
            / KEY_DIM**0.5
        )
        taylor = 1.0 + scores + 0.5 * scores * scores
        row_ids = low + jnp.arange(block, dtype=jnp.int32)[:, None]
        col_ids = jnp.arange(high, dtype=jnp.int32)[None, :]
        taylor = jnp.where((col_ids <= row_ids)[None], taylor, 0.0)
        denom = denom_pre[low:high] + jnp.transpose(jnp.sum(taylor, axis=-1))
        numer_in = jnp.einsum(
            "hqk,khv->qhv",
            taylor.astype(jnp.bfloat16),
            val_rows[:high],
            preferred_element_type=jnp.float32,
        )
        numer = numer_pre[low:high] + numer_in
        outputs.append((numer / denom[..., None]).astype(jnp.bfloat16))
    attended = jnp.concatenate(outputs, axis=0).reshape(tok_rows, heads_here * VALUE_DIM)
    groups = lax.axis_size("head")
    width_here = D // groups
    out_cols = lax.dynamic_slice_in_dim(w_out, lax.axis_index("head") * width_here, width_here, 1)
    summed = jnp.dot(
        lax.all_gather(attended, "head", axis=1, tiled=True),
        out_cols,
        preferred_element_type=jnp.float32,
    )
    return summed.astype(jnp.bfloat16)


def solution(mesh):
    in_specs = (P("seq", None), P(None, "head"), P(None, "head"), P(None, "head"), P())
    out_specs = P("seq", "head")
    return jax.shard_map(
        per_device, mesh=mesh, in_specs=in_specs, out_specs=out_specs, check_vma=False
    )
```

profile of v0, /device:TPU:25, one launch (start us, length us, event | category | flops | bytes accessed | tf_op | source)
XLA Modules:
  0.0 233.9 jit_solution(3371781160244066553)
XLA Ops:
  7.6 3.9 %convolution_convert_fusion.2 = bf16[1024,128]{0,1:T(8,128)(2,1)S(1)} fusion(bf16[1024,2048]{1,0:T(8,128)(2,1)} %param.16, bf16[2048,128]{1,0:T(8,128)(2,1)S(1)} %copy-done), kind=kOutput, calls=%fused_computation.42 | convolution fusion | flops 537001984 | bytes 4980736 | tf_op jit(solution)/shard_map/dot_general | solution.py:59
  11.6 7.0 %convolution_convert_fusion = bf16[1024,1024]{0,1:T(8,128)(2,1)S(1)} fusion(bf16[1024,2048]{1,0:T(8,128)(2,1)S(1)} %copy-done.2, bf16[2048,1024]{1,0:T(8,128)(2,1)} %param.19), kind=kOutput, calls=%fused_computation.40 | convolution fusion | flops 4296015872 | bytes 10485760 | tf_op jit(solution)/shard_map/dot_general | solution.py:64
  18.6 1.3 multiply_convert_fusion.1
  19.9 2.0 copy-done.3
  22.0 1.7 fusion.10
  26.9 4.3 %convert_reduce_fusion = f32[8,273]{1,0:T(8,128)S(1)} fusion(bf16[1024,8,256]{0,2,1:T(8,128)(2,1)} %bitcast.80, bf16[1024,8,16]{0,2,1:T(8,128)(2,1)S(1)} %multiply_convert_fusion.3, bf16[273]{0:T(512)(128)(2,1)S(1)} %pad.5.clone), kind=kLoop, calls=%fused_computation.10 | loop fusion | flops 15652728 | bytes 4465730 | tf_op jit(solution)/shard_map/reduce_sum | solution.py:71
  32.7 2.3 slice.59
  34.9 4.0 %convolution_convert_fusion.1 = bf16[1024,128]{0,1:T(8,128)(2,1)S(1)} fusion(bf16[1024,2048]{1,0:T(8,128)(2,1)} %param.16, bf16[2048,128]{1,0:T(8,128)(2,1)S(1)} %copy-done.7), kind=kOutput, calls=%fused_computation.41 | convolution fusion | flops 537001984 | bytes 4980736 | tf_op jit(solution)/shard_map/dot_general | solution.py:54
  39.0 1.4 multiply_convert_fusion
  40.4 2.9 %copy.35 = bf16[1024,8,16,16]{0,1,3,2:T(8,128)(2,1)S(1)} copy(bf16[1024,8,16,16]{0,3,2,1:T(8,128)(2,1)S(1)} %multiply_convert_fusion) | data formatting | bytes 8388608 | tf_op jit(solution)/shard_map/convert.4
  43.6 2.9 %pad_maximum_fusion.1 = bf16[1024,8,273]{0,1,2:T(8,128)(2,1)} fusion(bf16[1024,8,256]{0,1,2:T(8,128)(2,1)S(1)} %bitcast.81, bf16[1024,8,16]{0,1,2:T(8,128)(2,1)S(1)} %copy.37, bf16[273]{0:T(512)(128)(2,1)S(1)} %pad.5.clone), kind=kLoop, calls=%fused_computation.19 | loop fusion | flops 4472832 | bytes 8929826 | tf_op jit(solution)/shard_map/concatenate | solution.py:30
  46.4 3.1 %gather_fusion.4 = bf16[153,1024,8]{1,2,0:T(8,128)(2,1)S(1)} fusion(bf16[1024,8,273]{0,1,2:T(8,128)(2,1)} %pad_maximum_fusion.1, s32[1024]{0:T(1024)S(1)} %pad_clamp_fusion.1), kind=kCustom, calls=%fused_computation.4 | custom fusion | bytes 5014116 | tf_op jit(solution)/shard_map/gather | solution.py:81
  49.7 31.8 %all_gather.12 = f32[16,8,153]{2,1,0:T(8,128)} all-gather(f32[1,8,153]{2,1,0:T(8,128)S(1)} %copy.33), channel_id=1, replica_groups=mesh['seq'=16,'head'=2] {'seq'}, dimensions={0}, use_global_device_ids=true | all-gather | bytes 83232 | tf_op jit(solution)/shard_map/all_gather | solution.py:14
  82.1 4.7 %fusion.3 = (f32[8,512]{1,0:T(8,128)S(1)}, f32[8,512,512]{1,2,0:T(8,128)}) fusion(pred[512,512]{0,1:T(8,128)(4,1)S(1)} %iota_compare_fusion.1, bf16[512,8,16]{0,2,1:T(8,128)(2,1)S(1)} %bitcast.93, bf16[512,8,16]{0,2,1:T(8,128)(2,1)S(1)} %bitcast.86), kind=kOutput, calls=%fused_computation.16 | convolution fusion | flops 81784832 | bytes 8929280 | tf_op jit(solution)/shard_map/qhd,khd->hqk/dot_general | solution.py:95
  86.7 7.8 %fusion.41 = (f32[8,512]{1,0:T(8,128)S(1)}, bf16[8,512,1024]{2,1,0:T(8,128)(2,1)}) fusion(bf16[512,8,16]{0,2,1:T(8,128)(2,1)S(1)} %bitcast.92, bf16[1024,8,16]{0,2,1:T(8,128)(2,1)S(1)} %bitcast.85, pred[512,1024]{1,0:T(8,128)(4,1)S(1)} %iota_compare_fusion), kind=kOutput, calls=%fused_computation.65 | convolution fusion | flops 167768064 | bytes 9322496 | tf_op jit(solution)/shard_map/qhd,khd->hqk/dot_general | solution.py:95
  94.6 60.3 %all-gather.3.cloned.1.call-done = f32[16,8,153,128]{3,1,2,0:T(8,128)} async-done(((f32[1,8,153,128]{3,1,2,0:T(8,128)}), f32[16,8,153,128]{3,1,2,0:T(8,128)}) %all-gather.3.cloned.1.call-update) | async-done | bytes 10027024 | tf_op jit(solution)/shard_map/all_gather | solution.py:14
  154.9 24.6 %while.12 = (s32[]{:T(128)}, f32[8,153,128]{2,1,0:T(8,128)S(1)}, f32[8,153]{1,0:T(8,128)S(1)}, s32[]{:T(128)}, f32[16,8,153,128]{3,1,2,0:T(8,128)}, /*index=5*/f...) while((s32[]{:T(128)}, f32[8,153,128]{2,1,0:T(8,128)S(1)}, f32[8,153]{1,0:T(8,128)S(1)}, s32[]{:T(128)}, ...), condition=%wide.region_2.3_spmd, body=%wide.region_1.2_spmd.sunk | while | flops 157901 | bytes 3148271 | solution.py:22
  179.5 3.1 %fusion.16 = f32[1024,8,128]{0,2,1:T(8,128)S(1)} fusion(bf16[1024,8,153]{0,1,2:T(8,128)(2,1)S(1)} %bitcast.77, f32[8,153,128]{2,1,0:T(8,128)S(1)} %get-tuple-element.39), kind=kOutput, calls=%fused_computation.30 | convolution fusion | flops 321020928 | bytes 7327744 | tf_op jit(solution)/shard_map/thf,hfv->thv/dot_general | solution.py:83
  182.6 3.6 %fusion.11 = f32[8,1,1024]{2,1,0:T(1,128)S(1)} fusion(bf16[1024,8,153]{0,1,2:T(8,128)(2,1)S(1)} %bitcast.78, f32[8,153,1]{1,0,2:T(8,128)S(1)} %bitcast.90), kind=kOutput, calls=%fused_computation.25 | convolution fusion | flops 15040512 | bytes 2544416 | tf_op jit(solution)/shard_map/thf,hf->th/dot_general | solution.py:86
  186.3 6.5 %fusion.20 = bf16[512,8,128]{0,2,1:T(8,128)(2,1)S(1)} fusion(f32[1024,8,128]{0,2,1:T(8,128)S(1)} %fusion.16, bf16[1024,8,128]{0,2,1:T(8,128)(2,1)S(1)} %bitcast.89, bf16[8,512,1024]{2,1,0:T(8,128)(2,1)} %get-tuple-element.78, f32[512,8]{0,1:T(8,128)S(1)} %get-tuple-element.74), kind=kOutput, calls=%fused_computation.33 | convolution fusion | flops 1075314688 | bytes 13647872 | tf_op jit(solution)/shard_map/hqk,khv->qhv/dot_general | solution.py:108
  192.8 2.6 %fusion.22 = bf16[512,8,128]{0,2,1:T(8,128)(2,1)S(1)} fusion(f32[1024,8,128]{0,2,1:T(8,128)S(1)} %fusion.16, bf16[512,8,128]{0,2,1:T(8,128)(2,1)S(1)} %bitcast.87, f32[8,512,512]{1,2,0:T(8,128)S(1)} %bitcast.95, pred[512,512]{0,1:T(8,128)(4,1)S(1)} %iota_compare_fusion.1, f32[512,8]{0,1:T(8,128)S(1)} %get-tuple-element.73), kind=kOutput, calls=%fused_computation.36 | convolution fusion | flops 553123840 | bytes 12861440 | tf_op jit(solution)/shard_map/hqk,khv->qhv/dot_general | solution.py:108
  195.4 1.6 pad_maximum_fusion.3
  197.1 20.6 %all-gather.5.cloned.1.call-done = bf16[1024,2048]{0,1:T(8,128)(2,1)} async-done(((bf16[1024,1024]{0,1:T(8,128)(2,1)}), bf16[1024,2048]{0,1:T(8,128)(2,1)}) %all-gather.5.cloned.1.call-update) | async-done | bytes 4194320 | tf_op jit(solution)/shard_map/all_gather | solution.py:121
  217.7 9.4 %fusion.23 = bf16[1024,1024]{1,0:T(8,128)(2,1)} fusion(bf16[1024,2048]{0,1:T(8,128)(2,1)} %all-gather.5.cloned.1.call-done, bf16[2048,2048]{1,0:T(8,128)(2,1)} %param.20, s32[]{:T(128)S(6)} %select_n.63), kind=kOutput, calls=%fused_computation.39 | convolution fusion | flops 4296015872 | bytes 10485764 | tf_op jit(solution)/shard_map/dot_general | solution.py:120
  (97 shorter events, 31.2 us)
Async XLA Ops:
  6.5 1.0 copy-start
  6.5 5.0 %copy-start.12 = (s32[153]{0:T(256)S(1)}, s32[153]{0:T(256)}, u32[]{:S(2)}) copy-start(s32[153]{0:T(256)} %constant.77) | copy-start | bytes 1840
  6.5 148.3 %all-gather.3.cloned.1.call-start = ((), (), s32[]{:S(2)}) async-start(), calls=%async_computation | async-start | bytes 10653696 | tf_op jit(solution)/shard_map/all_gather | solution.py:14
  7.6 4.0 %copy-start.2 = (bf16[1024,2048]{1,0:T(8,128)(2,1)S(1)}, bf16[1024,2048]{1,0:T(8,128)(2,1)}, u32[]{:S(2)}) copy-start(bf16[1024,2048]{1,0:T(8,128)(2,1)} %param.16) | copy-start | bytes 12582916
  11.4 21.2 %copy-start.4 = (bf16[1024,128]{0,1:T(8,128)(2,1)}, bf16[1024,128]{0,1:T(8,128)(2,1)S(1)}, u32[]{:S(2)}) copy-start(bf16[1024,128]{0,1:T(8,128)(2,1)S(1)} %convolution_convert_fusion.2) | copy-start | bytes 786436
  18.6 5.0 %copy-start.8 = (bf16[1024,1024]{0,1:T(8,128)(2,1)}, bf16[1024,1024]{0,1:T(8,128)(2,1)S(1)}, u32[]{:S(2)}) copy-start(bf16[1024,1024]{0,1:T(8,128)(2,1)S(1)} %convolution_convert_fusion) | copy-start | bytes 6291460
  19.9 2.1 copy-start.3
  22.0 1.9 copy-start.11
  23.6 1.9 copy-start.10
  26.6 8.3 %copy-start.7 = (bf16[2048,128]{1,0:T(8,128)(2,1)S(1)}, bf16[2048,128]{1,0:T(8,128)(2,1)}, u32[]{:S(2)}) copy-start(bf16[2048,128]{1,0:T(8,128)(2,1)} %param.17) | copy-start | bytes 1572868
  26.7 191.0 %all-gather.5.cloned.1.call-start = ((), (), s32[]{:S(2)}) async-start(), calls=%async_computation.1 | async-start | bytes 6291456 | tf_op jit(solution)/shard_map/all_gather | solution.py:121
  46.4 35.6 %slice-start = ((bf16[1024,128]{0,1:T(8,128)(2,1)}), bf16[512,128]{0,1:T(8,128)(2,1)S(1)}, s32[]{:S(2)}) async-start(bf16[1024,128]{0,1:T(8,128)(2,1)} %copy-done.4), calls=%async_computation.2 | async-start | bytes 262144 | tf_op jit(solution)/shard_map/slice | solution.py:98
  82.1 4.7 %copy-start.5 = (bf16[1024,128]{0,1:T(8,128)(2,1)S(1)}, bf16[1024,128]{0,1:T(8,128)(2,1)}, u32[]{:S(2)}) copy-start(bf16[1024,128]{0,1:T(8,128)(2,1)} %copy-done.4) | copy-start | bytes 786436
  179.5 6.7 %copy-start.9 = (bf16[1024,1024]{0,1:T(8,128)(2,1)S(1)}, bf16[1024,1024]{0,1:T(8,128)(2,1)}, u32[]{:S(2)}) copy-start(bf16[1024,1024]{0,1:T(8,128)(2,1)} %copy-done.8) | copy-start | bytes 6291460
  182.6 10.1 %slice-start.1 = ((s8[8388608]{0:T(1024)(128)(4,1)}), s8[4194304]{0:T(1024)(128)(4,1)S(1)}, s32[]{:S(2)}) async-start(s8[8388608]{0:T(1024)(128)(4,1)} %bitcast.94), calls=%async_computation.3 | async-start | bytes 8388608
  186.2 6.5 %copy-start.6 = (bf16[512,1024]{0,1:T(8,128)(2,1)S(1)}, bf16[512,1024]{0,1:T(8,128)(2,1)}, u32[]{:S(2)}) copy-start(bf16[512,1024]{0,1:T(8,128)(2,1)} %slice.59) | copy-start | bytes 3145732
  186.2 6.5 %slice-start.2 = ((s8[8388608]{0:T(1024)(128)(4,1)}), s8[4194304]{0:T(1024)(128)(4,1)S(1)}, s32[]{:S(2)}) async-start(s8[8388608]{0:T(1024)(128)(4,1)} %bitcast.94), calls=%async_computation.4 | async-start | bytes 8388608
  217.7 9.4 %copy-start.1 = (bf16[2048,128]{1,0:T(8,128)(2,1)S(1)}, bf16[2048,128]{1,0:T(8,128)(2,1)}, u32[]{:S(2)}) copy-start(bf16[2048,128]{1,0:T(8,128)(2,1)} %param.18) | copy-start | bytes 1572868
Sparse Core Ops, SparseCore 0:
  26.8 128.0 all-gather.2
  197.2 20.4 all-gather.4
where the time goes:
time: 237 us; the launch traced here: 234 us
  waiting for transfers between devices  80.9 us (34%)
  matrix products  54.2 us (23%)
  blocking collectives  31.8 us (13%)
  local copies, waits for them, and re-layouts  28.5 us (12%)
  other arithmetic  24.3 us (10%)
  between operations  13.8 us (6%)
    all_gather x1, waiting for transfers between devices, entering(): gathered = jax.tree.map(lambda a: lax.all_gather(a, axis), part)  60.3 us
    all_gather x1, blocking collectives, entering(): gathered = jax.tree.map(lambda a: lax.all_gather(a, axis), part)  31.8 us
    all_gather x1, waiting for transfers between devices, per_device(): lax.all_gather(attended, 'head', axis=1, tiled=True)  20.6 us
    dynamic_slice x12, local copies, waits for them, and re-layouts, one(): lax.dynamic_index_in_dim(a, lap, 0, False)  13.4 us
    dot_general x2, matrix products, per_device(): jnp.einsum('qhd,khd->hqk', queries[low:high], key_rows[:high], preferred_...  12.5 us
    add x24, other arithmetic, add_pair(): return (earlier[0] + later[0], earlier[1] + later[1])  11 us
    dot_general x1, matrix products, per_device(): jnp.dot(lax.all_gather(attended, 'head', axis=1, tiled=True), out_cols, p...  9.41 us
    dot_general x2, matrix products, per_device(): jnp.einsum('hqk,khv->qhv', taylor.astype(jnp.bfloat16), val_rows[:high],...  9.12 us
  transfers between devices with their start and end apart: 2, of which 2 were waited for; matrix products, arithmetic and copies ran while one was open for 15% of the time, Pallas kernels for 0%

commit v1 on v0

v1 whole, which is shorter than its diff:
```python
import functools

import jax
import jax.numpy as jnp
from jax import lax
from jax.experimental import pallas as pl
from jax.experimental.pallas import tpu as pltpu
from jax.sharding import PartitionSpec as P

KEY_DIM = 16
VALUE_DIM = 128
ROWS = 160
PAIR = 2
MESH = pl.DeviceIdType.MESH
F32 = jnp.float32
BF16 = jnp.bfloat16


def features(u, tail_one, square):
    n = u.shape[1]
    twice = jnp.concatenate([u, u], axis=0)
    parts = [u, u * u * square]
    for d in range(1, KEY_DIM // 2):
        parts.append(u * twice[d : d + KEY_DIM])
    half = KEY_DIM // 2
    parts.append(u[:half] * u[half:])
    row = lax.broadcasted_iota(jnp.int32, (8, n), 0)
    parts.append(jnp.where(row == 0, tail_one, 0.0))
    return jnp.concatenate(parts, axis=0)


def pack_norm(total):
    state, norm = total[:, :VALUE_DIM], total[:, VALUE_DIM:]
    top = norm[:VALUE_DIM]
    rest = norm[VALUE_DIM:]

    def diagonal(block):
        r = lax.broadcasted_iota(jnp.int32, block.shape, 0)
        l = lax.broadcasted_iota(jnp.int32, block.shape, 1)
        return jnp.sum(jnp.where(r == l, block, 0.0), axis=0, keepdims=True)

    first, second = diagonal(top), diagonal(rest)
    r = lax.broadcasted_iota(jnp.int32, (8, VALUE_DIM), 0)
    tail = jnp.where(r == 0, state[ROWS - 8 :], jnp.where(r == 1, first, jnp.where(r == 2, second, 0.0)))
    return jnp.concatenate([state[: ROWS - 8], tail], axis=0)


def unpack_norm(packed):
    tail = packed[ROWS - 8 :]

    def column(row, height):
        r = lax.broadcasted_iota(jnp.int32, (height, VALUE_DIM), 0)
        l = lax.broadcasted_iota(jnp.int32, (height, VALUE_DIM), 1)
        return jnp.sum(jnp.where(r == l, row, 0.0), axis=1, keepdims=True)

    return jnp.concatenate([column(tail[1:2], VALUE_DIM), column(tail[2:3], ROWS - VALUE_DIM)], axis=0)


def kernel(
    n_seq, chunk,
    tok_hbm, wq_hbm, wk_hbm, wv_hbm, wo_hbm, out_ref,
    tok, wqk, wv, wo, vals, qs, qt, kt, local, inner, qfeat, att,
    own, base, plane, send_x, recv_x, send_y, recv_y, send_z, recv_z,
    load_sem, x_ss, x_rs, y_ss, y_rs, z_ss, z_rs, a_ss, a_rs,
):
    rows, width = tok.shape
    heads = vals.shape[0]
    groups = heads // PAIR
    chunks = rows // chunk
    cols_here = wo.shape[1]
    chain = n_seq // 4
    seq = lax.axis_index("seq")
    core = lax.axis_index("head")
    x = lax.rem(seq, 2)
    y = lax.rem(seq // 2, 2)
    z = seq // 4
    x_peer = seq + 1 - 2 * x
    y_peer = seq + 2 - 4 * y
    up = lax.rem(seq + 4, n_seq)
    down = lax.rem(seq + n_seq - 4, n_seq)

    load_qk = [
        pltpu.make_async_copy(wq_hbm, wqk.at[:, pl.ds(0, 128)], load_sem.at[0]),
        pltpu.make_async_copy(wk_hbm, wqk.at[:, pl.ds(128, 128)], load_sem.at[1]),
        pltpu.make_async_copy(tok_hbm, tok, load_sem.at[2]),
    ]
    load_v = pltpu.make_async_copy(wv_hbm, wv, load_sem.at[3])
    load_o = pltpu.make_async_copy(
        wo_hbm.at[:, pl.ds(pl.multiple_of(core * cols_here, 128), cols_here)], wo, load_sem.at[4]
    )
    for c in load_qk:
        c.start()
    load_v.start()

    barrier = pltpu.get_barrier_semaphore()
    for peer in (x_peer, y_peer, up, down):
        pl.semaphore_signal(barrier, inc=1, device_id=(peer, core), device_id_type=MESH)
    pl.semaphore_signal(barrier, inc=1, device_id=(seq, 1 - core), device_id_type=MESH)
    pl.semaphore_wait(barrier, 5)

    def copy_x(g):
        return pltpu.make_async_remote_copy(
            src_ref=send_x.at[g], dst_ref=recv_x.at[g], send_sem=x_ss.at[g], recv_sem=x_rs.at[g],
            device_id=(x_peer, core), device_id_type=MESH)

    def copy_y(g):
        return pltpu.make_async_remote_copy(
            src_ref=send_y.at[g], dst_ref=recv_y.at[g], send_sem=y_ss.at[g], recv_sem=y_rs.at[g],
            device_id=(y_peer, core), device_id_type=MESH)

    def copy_z(g):
        return pltpu.make_async_remote_copy(
            src_ref=send_z.at[g], dst_ref=recv_z.at[g], send_sem=z_ss.at[g], recv_sem=z_rs.at[g],
            device_id=(up, core), device_id_type=MESH)

    def copy_a(g):
        at = pl.ds(pl.multiple_of(core * (heads * VALUE_DIM) + g * (PAIR * VALUE_DIM), 128), PAIR * VALUE_DIM)
        return pltpu.make_async_remote_copy(
            src_ref=att.at[:, at], dst_ref=att.at[:, at], send_sem=a_ss.at[g], recv_sem=a_rs.at[g],
            device_id=(seq, 1 - core), device_id_type=MESH)

    def pump(t):
        gx, gy, gz = t - 1, t - 2, t - 2 - z

        @pl.when((gx >= 0) & (gx < groups))
        def _():
            copy_x(gx).wait_recv()
            other = recv_x[gx].astype(F32)
            both = own[gx] + other
            send_y[gx] = both.astype(BF16)
            copy_y(gx).start()
            plane[gx] = both
            base[gx] = jnp.where(x == 1, other, 0.0)

        @pl.when((gy >= 0) & (gy < groups))
        def _():
            copy_y(gy).wait_recv()
            other = recv_y[gy].astype(F32)
            plane[gy] = plane[gy] + other
            base[gy] = base[gy] + jnp.where(y == 1, other, 0.0)

        @pl.when((gz >= 0) & (gz < groups))
        def _():
            @pl.when(z > 0)
            def _():
                copy_z(gz).wait_recv()
                earlier = recv_z[gz].astype(F32)
                base[gz] = base[gz] + earlier
                plane[gz] = plane[gz] + earlier

            @pl.when(z < chain - 1)
            def _():
                send_z[gz] = plane[gz].astype(BF16)
                copy_z(gz).start()

    for c in load_qk:
        c.wait()
    load_o.start()
    qk = jnp.dot(tok[...], wqk[...], preferred_element_type=F32).astype(BF16).astype(F32)
    q = qk[:, :128] * 0.25
    qs[...] = q.astype(BF16)
    qt[...] = q.T
    kt[...] = qk[:, 128:].T
    load_v.wait()

    def head_rows(h):
        return pl.ds(pl.multiple_of(h * KEY_DIM, KEY_DIM), KEY_DIM)

    def group_step(g, _):
        at = pl.ds(pl.multiple_of(g * (PAIR * VALUE_DIM), 128), PAIR * VALUE_DIM)
        v = jnp.dot(tok[...], wv[:, at], preferred_element_type=F32).astype(BF16)
        for i in range(PAIR):
            vals[g * PAIR + i] = v[:, i * VALUE_DIM : (i + 1) * VALUE_DIM]
        ones = jnp.ones((chunk, VALUE_DIM), BF16)
        for i in range(PAIR):
            h = g * PAIR + i
            total = jnp.zeros((ROWS, 2 * VALUE_DIM), F32)
            for c in range(chunks):
                local[h, c] = total
                feat = features(kt[head_rows(h), pl.ds(c * chunk, chunk)], 1.0, 1.0).astype(BF16)
                wide = jnp.concatenate([vals[h, pl.ds(c * chunk, chunk)], ones], axis=1)
                total = total + jnp.dot(feat, wide, preferred_element_type=F32)
            packed = pack_norm(total)
            own[g, i] = packed
            send_x[g, i] = packed.astype(BF16)
        copy_x(g).start()
        pump(g)
        return 0

    lax.fori_loop(0, groups, group_step, 0)

    def inner_step(h, _):
        row_head = lax.broadcasted_iota(jnp.int32, (128, chunk), 0) // KEY_DIM
        r = lax.broadcasted_iota(jnp.int32, (chunk, chunk), 0)
        l = lax.broadcasted_iota(jnp.int32, (chunk, chunk), 1)
        ones = jnp.ones((chunk, VALUE_DIM), BF16)
        for c in range(chunks):
            span = pl.ds(c * chunk, chunk)
            k_own = jnp.where(row_head == h, kt[:, span], 0.0).astype(BF16)
            s = jnp.dot(qs[span], k_own, preferred_element_type=F32)
            s1 = s + 1.0
            taylor = jnp.where(l <= r, 0.5 * (s1 * s1) + 0.5, 0.0).astype(BF16)
            wide = jnp.concatenate([vals[h, span], ones], axis=1)
            inner[h, span] = jnp.dot(taylor, wide, preferred_element_type=F32)
            feat = features(qt[head_rows(h), span], 1.0, 0.5)
            qfeat[h, span] = feat.T.astype(BF16)
        pump(groups + h)
        return 0

    lax.fori_loop(0, heads, inner_step, 0)

    def rest(t, _):
        pump(t)
        return 0

    lax.fori_loop(groups + heads, max(groups + heads, groups + chain + 2), rest, 0)

    def outer_step(g, _):
        for i in range(PAIR):
            h = g * PAIR + i
            packed = base[g, i]
            norm = jnp.broadcast_to(unpack_norm(packed), (ROWS, VALUE_DIM))
            entering = jnp.concatenate([packed, norm], axis=1)
            for c in range(chunks):
                span = pl.ds(c * chunk, chunk)
                prefix = (entering + local[h, c]).astype(BF16)
                total = inner[h, span] + jnp.dot(qfeat[h, span], prefix, preferred_element_type=F32)
                result = total[:, :VALUE_DIM] / total[:, VALUE_DIM:]
                at = pl.ds(pl.multiple_of(core * (heads * VALUE_DIM) + h * VALUE_DIM, 128), VALUE_DIM)
                att[span, at] = result.astype(BF16)
        copy_a(g).start()
        return 0

    lax.fori_loop(0, groups, outer_step, 0)
    load_o.wait()

    def await_peer(g, _):
        at = pl.ds(pl.multiple_of((1 - core) * (heads * VALUE_DIM) + g * (PAIR * VALUE_DIM), 128), PAIR * VALUE_DIM)
        pltpu.make_async_remote_copy(
            src_ref=att.at[:, at], dst_ref=att.at[:, at], send_sem=a_ss.at[g], recv_sem=a_rs.at[g],
            device_id=(seq, 1 - core), device_id_type=MESH).wait_recv()
        return 0

    lax.fori_loop(0, groups, await_peer, 0)

    def out_step(b, _):
        at = pl.ds(pl.multiple_of(b * 256, 128), 256)
        out_ref[:, at] = jnp.dot(att[...], wo[:, at], preferred_element_type=F32).astype(BF16)
        return 0

    lax.fori_loop(0, cols_here // 256, out_step, 0)

    def finish(g, _):
        copy_x(g).wait_send()
        copy_y(g).wait_send()
        copy_a(g).wait_send()

        @pl.when(z < chain - 1)
        def _():
            copy_z(g).wait_send()

        return 0

    lax.fori_loop(0, groups, finish, 0)


def per_device(tokens, w_query, w_key, w_value, w_out):
    n_seq = lax.axis_size("seq")
    rows, width = tokens.shape
    heads = w_query.shape[1] // KEY_DIM
    groups = heads // PAIR
    chunk = min(256, rows)
    cols = w_out.shape[1] // lax.axis_size("head")
    vm = pltpu.VMEM
    slot = (groups, PAIR, ROWS, VALUE_DIM)
    dma = pltpu.SemaphoreType.DMA
    return pl.pallas_call(
        functools.partial(kernel, n_seq, chunk),
        out_shape=jax.ShapeDtypeStruct((rows, cols), BF16),
        in_specs=[pl.BlockSpec(memory_space=pl.ANY)] * 5,
        out_specs=pl.BlockSpec(memory_space=pltpu.VMEM),
        scratch_shapes=[
            vm((rows, width), BF16),
            vm((width, 256), BF16),
            vm(w_value.shape, BF16),
            vm((w_out.shape[0], cols), BF16),
            vm((heads, rows, VALUE_DIM), BF16),
            vm((rows, 128), BF16),
            vm((128, rows), F32),
            vm((128, rows), F32),
            vm((heads, rows // chunk, ROWS, 2 * VALUE_DIM), F32),
            vm((heads, rows, 2 * VALUE_DIM), F32),
            vm((heads, rows, ROWS), BF16),
            vm((rows, w_out.shape[0]), BF16),
            vm(slot, F32), vm(slot, F32), vm(slot, F32),
            vm(slot, BF16), vm(slot, BF16), vm(slot, BF16), vm(slot, BF16), vm(slot, BF16), vm(slot, BF16),
            dma((5,)),
            dma((groups,)), dma((groups,)), dma((groups,)), dma((groups,)), dma((groups,)), dma((groups,)),
            dma((groups,)), dma((groups,)),
        ],
        compiler_params=pltpu.CompilerParams(
            collective_id=0, has_side_effects=True, vmem_limit_bytes=62 * 1024 * 1024
        ),
    )(tokens, w_query, w_key, w_value, w_out)


def solution(mesh):
    in_specs = (P("seq", None), P(None, "head"), P(None, "head"), P(None, "head"), P())
    return jax.shard_map(
        per_device, mesh=mesh, in_specs=in_specs, out_specs=P("seq", "head"), check_vma=False
    )
```

time: 237 us -> 48.7 us (0.21); the launches traced: 234 us -> 48.6 us
  waiting for transfers between devices: 80.9 us -> 0 us
  matrix products: 54.2 us -> 0 us
  Pallas kernels: 0 us -> 45.5 us
  blocking collectives: 31.8 us -> 0 us
  local copies, waits for them, and re-layouts: 28.5 us -> 3.08 us
  other arithmetic: 24.3 us -> 0 us
  between operations: 13.8 us -> 0.01 us
    all_gather x2 -> x0, waiting for transfers between devices: 80.9 us -> none  [the longest x1 60.3 us: entering(): gathered = jax.tree.map(lambda a: lax.all_gather(a, axis), part)]
    dot_general x11 -> x0, matrix products: 54.2 us -> none  [the longest x2 12.5 us: per_device(): jnp.einsum('qhd,khd->hqk', queries[low:high], key_rows[:high], preferred_...]
    pallas_call x0 -> x1, Pallas kernels: none -> 45.5 us  [per_device(): pl.pallas_call(functools.partial(kernel, n_seq, chunk), out_shape=jax.Sha...]
    all_gather x1 -> x0, blocking collectives: 31.8 us -> none  [entering(): gathered = jax.tree.map(lambda a: lax.all_gather(a, axis), part)]
    dynamic_slice x12 -> x0, local copies, waits for them, and re-layouts: 13.4 us -> none  [one(): lax.dynamic_index_in_dim(a, lap, 0, False)]
    add x28 -> x0, other arithmetic: 12.2 us -> none  [the longest x24 11 us: add_pair(): return (earlier[0] + later[0], earlier[1] + later[1])]
    gather x5 -> x0, local copies, waits for them, and re-layouts: 6.11 us -> none  [the longest x1 3.14 us: per_device(): used_feat = query_feat[:, :, kept_rows]]
    concatenate x2 -> x0, other arithmetic: 4.47 us -> none  [the longest x1 2.87 us: taylor_features(): jnp.concatenate([ones, wide / count ** 0.25, outer / (2.0 * count) ** 0.5...]
  transfers between devices with their start and end apart: 2 -> 0, of which waited for: 2 -> 0; matrix products, arithmetic and copies ran while one was open for 15% -> 0% of each run, Pallas kernels for 0% -> 0%
where the time goes in v1:
time: 48.7 us; the launch traced here: 48.6 us
  Pallas kernels  45.5 us (93%)
  local copies, waits for them, and re-layouts  3.08 us (6%)
    pallas_call x1, Pallas kernels, per_device(): pl.pallas_call(functools.partial(kernel, n_seq, chunk), out_shape=jax.Sha...  45.5 us
    unnamed x1, local copies, waits for them, and re-layouts  3.08 us

profile of v1, /device:TPU:25, one launch (start us, length us, event | category | flops | bytes accessed | tf_op | source)
XLA Modules:
  0.0 48.6 jit_solution(12732126684880716934)
XLA Ops:
  0.0 45.5 %shard_map.55 = bf16[1024,1024]{1,0:T(8,128)(2,1)} custom-call(bf16[1024,2048]{1,0:T(8,128)(2,1)} %tok_hbm.1, bf16[2048,128]{1,0:T(8,128)(2,1)} %wq_hbm.1, bf16[2048,128]{1,0:T(8,128)(2,1)} %wk_hbm.1, bf16[2048,1024]{1,0:T(8,128)(2,1)} %wv_hbm.1, bf16[2048,2048]{1,0:T(8,128)(2,1)} %wo_hbm.1), custom_call_target="tpu_custom_call" | custom-call | tf_op jit(solution)/shard_map/pallas_call | solution.py:277
  45.5 3.1 %copy.7 = bf16[1024,1024]{1,0:T(8,128)(2,1)} copy(bf16[1024,1024]{1,0:T(8,128)(2,1)} %shard_map.55) | data formatting | bytes 4194304

commit v2 on v1

--- a/solution.py
+++ b/solution.py
@@ -11,6 +11,7 @@
 VALUE_DIM = 128
 ROWS = 160
 PAIR = 2
+LOADS = 2
 MESH = pl.DeviceIdType.MESH
 F32 = jnp.float32
 BF16 = jnp.bfloat16
@@ -61,7 +62,7 @@
     tok_hbm, wq_hbm, wk_hbm, wv_hbm, wo_hbm, out_ref,
     tok, wqk, wv, wo, vals, qs, qt, kt, local, inner, qfeat, att,
     own, base, plane, send_x, recv_x, send_y, recv_y, send_z, recv_z,
-    load_sem, x_ss, x_rs, y_ss, y_rs, z_ss, z_rs, a_ss, a_rs,
+    acc, load_sem, tok_sem, v_sem, x_ss, x_rs, y_ss, y_rs, z_ss, z_rs, a_ss, a_rs,
 ):
     rows, width = tok.shape
     heads = vals.shape[0]
@@ -79,24 +80,34 @@
     up = lax.rem(seq + 4, n_seq)
     down = lax.rem(seq + n_seq - 4, n_seq)
 
-    load_qk = [
+    half = rows // LOADS
+    load_w = [
+        pltpu.make_async_copy(wk_hbm, wqk.at[:, pl.ds(128, 128)], load_sem.at[1]),
         pltpu.make_async_copy(wq_hbm, wqk.at[:, pl.ds(0, 128)], load_sem.at[0]),
-        pltpu.make_async_copy(wk_hbm, wqk.at[:, pl.ds(128, 128)], load_sem.at[1]),
-        pltpu.make_async_copy(tok_hbm, tok, load_sem.at[2]),
     ]
-    load_v = pltpu.make_async_copy(wv_hbm, wv, load_sem.at[3])
+    load_t = [
+        pltpu.make_async_copy(tok_hbm.at[pl.ds(i * half, half)], tok.at[pl.ds(i * half, half)], tok_sem.at[i])
+        for i in range(LOADS)
+    ]
     load_o = pltpu.make_async_copy(
-        wo_hbm.at[:, pl.ds(pl.multiple_of(core * cols_here, 128), cols_here)], wo, load_sem.at[4]
+        wo_hbm.at[:, pl.ds(pl.multiple_of(core * cols_here, 128), cols_here)], wo, load_sem.at[2]
     )
-    for c in load_qk:
+
+    def load_v(g):
+        at = pl.ds(pl.multiple_of(g * (PAIR * VALUE_DIM), 128), PAIR * VALUE_DIM)
+        return pltpu.make_async_copy(wv_hbm.at[:, at], wv.at[:, at], v_sem.at[g])
+
+    for c in load_w:
         c.start()
-    load_v.start()
+    for c in load_t:
+        c.start()
+    for g in range(groups):
+        load_v(g).start()
 
     barrier = pltpu.get_barrier_semaphore()
     for peer in (x_peer, y_peer, up, down):
         pl.semaphore_signal(barrier, inc=1, device_id=(peer, core), device_id_type=MESH)
     pl.semaphore_signal(barrier, inc=1, device_id=(seq, 1 - core), device_id_type=MESH)
-    pl.semaphore_wait(barrier, 5)
 
     def copy_x(g):
         return pltpu.make_async_remote_copy(
@@ -120,9 +131,9 @@
             device_id=(seq, 1 - core), device_id_type=MESH)
 
     def pump(t):
-        gx, gy, gz = t - 1, t - 2, t - 2 - z
-
-        @pl.when((gx >= 0) & (gx < groups))
+        gx, gy, gz = t - 3, t - 6, t - 6 - 3 * z
+
+        @pl.when((gx >= 0) & (gx < heads))
         def _():
             copy_x(gx).wait_recv()
             other = recv_x[gx].astype(F32)
@@ -132,14 +143,14 @@
             plane[gx] = both
             base[gx] = jnp.where(x == 1, other, 0.0)
 
-        @pl.when((gy >= 0) & (gy < groups))
+        @pl.when((gy >= 0) & (gy < heads))
         def _():
             copy_y(gy).wait_recv()
             other = recv_y[gy].astype(F32)
             plane[gy] = plane[gy] + other
             base[gy] = base[gy] + jnp.where(y == 1, other, 0.0)
 
-        @pl.when((gz >= 0) & (gz < groups))
+        @pl.when((gz >= 0) & (gz < heads) & (z < chain - 1))
         def _():
             @pl.when(z > 0)
             def _():
@@ -148,26 +159,28 @@
                 base[gz] = base[gz] + earlier
                 plane[gz] = plane[gz] + earlier
 
-            @pl.when(z < chain - 1)
-            def _():
-                send_z[gz] = plane[gz].astype(BF16)
-                copy_z(gz).start()
-
-    for c in load_qk:
+            send_z[gz] = plane[gz].astype(BF16)
+            copy_z(gz).start()
+
+    for c in load_w:
         c.wait()
+    for i in range(LOADS):
+        load_t[i].wait()
+        part = pl.ds(i * half, half)
+        qk = jnp.dot(tok[part], wqk[...], preferred_element_type=F32).astype(BF16).astype(F32)
+        q = qk[:, :128] * 0.25
+        qs[part] = q.astype(BF16)
+        qt[:, part] = q.T
+        kt[:, part] = qk[:, 128:].T
     load_o.start()
-    qk = jnp.dot(tok[...], wqk[...], preferred_element_type=F32).astype(BF16).astype(F32)
-    q = qk[:, :128] * 0.25
-    qs[...] = q.astype(BF16)
-    qt[...] = q.T
-    kt[...] = qk[:, 128:].T
-    load_v.wait()
+    pl.semaphore_wait(barrier, 5)
 
     def head_rows(h):
         return pl.ds(pl.multiple_of(h * KEY_DIM, KEY_DIM), KEY_DIM)
 
     def group_step(g, _):
         at = pl.ds(pl.multiple_of(g * (PAIR * VALUE_DIM), 128), PAIR * VALUE_DIM)
+        load_v(g).wait()
         v = jnp.dot(tok[...], wv[:, at], preferred_element_type=F32).astype(BF16)
         for i in range(PAIR):
             vals[g * PAIR + i] = v[:, i * VALUE_DIM : (i + 1) * VALUE_DIM]
@@ -181,15 +194,15 @@
                 wide = jnp.concatenate([vals[h, pl.ds(c * chunk, chunk)], ones], axis=1)
                 total = total + jnp.dot(feat, wide, preferred_element_type=F32)
             packed = pack_norm(total)
-            own[g, i] = packed
-            send_x[g, i] = packed.astype(BF16)
-        copy_x(g).start()
-        pump(g)
+            own[h] = packed
+            send_x[h] = packed.astype(BF16)
+            copy_x(h).start()
+            pump(h)
         return 0
 
     lax.fori_loop(0, groups, group_step, 0)
 
-    def inner_step(h, _):
+    def inner_head(h):
         row_head = lax.broadcasted_iota(jnp.int32, (128, chunk), 0) // KEY_DIM
         r = lax.broadcasted_iota(jnp.int32, (chunk, chunk), 0)
         l = lax.broadcasted_iota(jnp.int32, (chunk, chunk), 1)
@@ -204,21 +217,35 @@
             inner[h, span] = jnp.dot(taylor, wide, preferred_element_type=F32)
             feat = features(qt[head_rows(h), span], 1.0, 0.5)
             qfeat[h, span] = feat.T.astype(BF16)
-        pump(groups + h)
-        return 0
-
-    lax.fori_loop(0, heads, inner_step, 0)
+
+    def inner_step(g, _):
+        for i in range(PAIR):
+            inner_head(g * PAIR + i)
+        pump(heads + g)
+        return 0
+
+    lax.fori_loop(0, groups, inner_step, 0)
+
+    first = heads + groups
+
+    def pumped(g):
+        return jnp.maximum(first + 1 + g, PAIR * (g + 1) + 6 + 3 * (chain - 2))
 
     def rest(t, _):
         pump(t)
         return 0
 
-    lax.fori_loop(groups + heads, max(groups + heads, groups + chain + 2), rest, 0)
-
-    def outer_step(g, _):
+    def outer_step(g):
+        lax.fori_loop(jnp.where(g == 0, first, pumped(g - 1)), pumped(g), rest, 0)
         for i in range(PAIR):
             h = g * PAIR + i
-            packed = base[g, i]
+
+            @pl.when(z == chain - 1)
+            def _():
+                copy_z(h).wait_recv()
+                base[h] = base[h] + recv_z[h].astype(F32)
+
+            packed = base[h]
             norm = jnp.broadcast_to(unpack_norm(packed), (ROWS, VALUE_DIM))
             entering = jnp.concatenate([packed, norm], axis=1)
             for c in range(chunks):
@@ -229,35 +256,54 @@
                 at = pl.ds(pl.multiple_of(core * (heads * VALUE_DIM) + h * VALUE_DIM, 128), VALUE_DIM)
                 att[span, at] = result.astype(BF16)
         copy_a(g).start()
-        return 0
-
-    lax.fori_loop(0, groups, outer_step, 0)
+
+    own_at, peer_at = core * (heads * VALUE_DIM), (1 - core) * (heads * VALUE_DIM)
+    step = PAIR * VALUE_DIM
+
+    def out_step(g, begin, end):
+        here = pl.ds(pl.multiple_of(own_at + g * step, 128), step)
+        there = pl.ds(pl.multiple_of(peer_at + g * step, 128), step)
+        pltpu.make_async_remote_copy(
+            src_ref=att.at[:, there], dst_ref=att.at[:, there], send_sem=a_ss.at[g], recv_sem=a_rs.at[g],
+            device_id=(seq, 1 - core), device_id_type=MESH).wait_recv()
+
+        def block(b, _):
+            at = pl.ds(pl.multiple_of(b * 256, 128), 256)
+            both = jnp.concatenate([att[:, here], att[:, there]], axis=1)
+            part = jnp.dot(both, jnp.concatenate([wo[here, at], wo[there, at]], axis=0), preferred_element_type=F32)
+            if not begin:
+                part = part + acc[:, at]
+            if end:
+                out_ref[:, at] = part.astype(BF16)
+            else:
+                acc[:, at] = part
+            return 0
+
+        lax.fori_loop(0, cols_here // 256, block, 0)
+
+    outer_step(0)
     load_o.wait()
-
-    def await_peer(g, _):
-        at = pl.ds(pl.multiple_of((1 - core) * (heads * VALUE_DIM) + g * (PAIR * VALUE_DIM), 128), PAIR * VALUE_DIM)
-        pltpu.make_async_remote_copy(
-            src_ref=att.at[:, at], dst_ref=att.at[:, at], send_sem=a_ss.at[g], recv_sem=a_rs.at[g],
-            device_id=(seq, 1 - core), device_id_type=MESH).wait_recv()
-        return 0
-
-    lax.fori_loop(0, groups, await_peer, 0)
-
-    def out_step(b, _):
-        at = pl.ds(pl.multiple_of(b * 256, 128), 256)
-        out_ref[:, at] = jnp.dot(att[...], wo[:, at], preferred_element_type=F32).astype(BF16)
-        return 0
-
-    lax.fori_loop(0, cols_here // 256, out_step, 0)
+    outer_step(1)
+    out_step(0, True, False)
+
+    def later(g, _):
+        outer_step(g)
+        out_step(g - 1, False, False)
+        return 0
+
+    lax.fori_loop(2, groups, later, 0)
+    out_step(groups - 1, False, True)
 
     def finish(g, _):
-        copy_x(g).wait_send()
-        copy_y(g).wait_send()
         copy_a(g).wait_send()
-
-        @pl.when(z < chain - 1)
-        def _():
-            copy_z(g).wait_send()
+        for i in range(PAIR):
+            h = g * PAIR + i
+            copy_x(h).wait_send()
+            copy_y(h).wait_send()
+
+            @pl.when(z < chain - 1)
+            def _():
+                copy_z(h).wait_send()
 
         return 0
 
@@ -272,7 +318,7 @@
     chunk = min(256, rows)
     cols = w_out.shape[1] // lax.axis_size("head")
     vm = pltpu.VMEM
-    slot = (groups, PAIR, ROWS, VALUE_DIM)
+    slot = (heads, ROWS, VALUE_DIM)
     dma = pltpu.SemaphoreType.DMA
     return pl.pallas_call(
         functools.partial(kernel, n_seq, chunk),
@@ -294,12 +340,13 @@
             vm((rows, w_out.shape[0]), BF16),
             vm(slot, F32), vm(slot, F32), vm(slot, F32),
             vm(slot, BF16), vm(slot, BF16), vm(slot, BF16), vm(slot, BF16), vm(slot, BF16), vm(slot, BF16),
-            dma((5,)),
-            dma((groups,)), dma((groups,)), dma((groups,)), dma((groups,)), dma((groups,)), dma((groups,)),
+            vm((rows, cols), F32),
+            dma((3,)), dma((LOADS,)), dma((groups,)),
+            dma((heads,)), dma((heads,)), dma((heads,)), dma((heads,)), dma((heads,)), dma((heads,)),
             dma((groups,)), dma((groups,)),
         ],
         compiler_params=pltpu.CompilerParams(
-            collective_id=0, has_side_effects=True, vmem_limit_bytes=62 * 1024 * 1024
+            collective_id=0, has_side_effects=True, vmem_limit_bytes=50 * 1024 * 1024
         ),
     )(tokens, w_query, w_key, w_value, w_out)
 

time: 48.7 us -> 40.9 us (0.84)
  Pallas kernels: 45.5 us -> 37.3 us
    pallas_call x1, Pallas kernels: 45.5 us -> 37.3 us  [per_device(): pl.pallas_call(functools.partial(kernel, n_seq, chunk), out_shape=jax.Sha...]
    unnamed x1 -> x5, local copies, waits for them, and re-layouts: 3.08 us -> 3.4 us
where the time goes in v2:
time: 40.9 us; the launch traced here: 40.7 us
  Pallas kernels  37.3 us (91%)
  local copies, waits for them, and re-layouts  3.4 us (8%)
    pallas_call x1, Pallas kernels, per_device(): pl.pallas_call(functools.partial(kernel, n_seq, chunk), out_shape=jax.Sha...  37.3 us
    unnamed x5, local copies, waits for them, and re-layouts  3.4 us

profile of v2, /device:TPU:25, one launch (start us, length us, event | category | flops | bytes accessed | tf_op | source)
XLA Modules:
  0.0 40.7 jit_solution(16304408626925299754)
XLA Ops:
  0.0 0.0 copy-start
  0.0 1.0 %copy-done = bf16[2048,128]{1,0:T(8,128)(2,1)S(1)} copy-done((bf16[2048,128]{1,0:T(8,128)(2,1)S(1)}, bf16[2048,128]{1,0:T(8,128)(2,1)}, u32[]{:S(2)}) %copy-start) | copy-done | bytes 524312
  1.0 0.0 copy-start.1
  1.0 1.0 %copy-done.1 = bf16[2048,128]{1,0:T(8,128)(2,1)S(1)} copy-done((bf16[2048,128]{1,0:T(8,128)(2,1)S(1)}, bf16[2048,128]{1,0:T(8,128)(2,1)}, u32[]{:S(2)}) %copy-start.1) | copy-done | bytes 524312
  2.1 37.3 %shard_map.55 = bf16[1024,1024]{1,0:T(8,128)(2,1)S(1)} custom-call(bf16[1024,2048]{1,0:T(8,128)(2,1)} %tok_hbm.1, bf16[2048,128]{1,0:T(8,128)(2,1)S(1)} %copy-done, bf16[2048,128]{1,0:T(8,128)(2,1)S(1)} %copy-done.1, bf16[2048,1024]{1,0:T(8,128)(2,1)} %wv_hbm.1, bf16[2048,2048]{1,0:T(8,128)(2,1)} %wo_hbm.1), custom_call_target="tpu_custom_call" | custom-call | tf_op jit(solution)/shard_map/pallas_call | solution.py:323
  39.4 1.3 %copy.7 = bf16[1024,1024]{1,0:T(8,128)(2,1)} copy(bf16[1024,1024]{1,0:T(8,128)(2,1)S(1)} %shard_map.55) | data formatting | bytes 4194304
Async XLA Ops:
  0.0 1.0 %copy-start = (bf16[2048,128]{1,0:T(8,128)(2,1)S(1)}, bf16[2048,128]{1,0:T(8,128)(2,1)}, u32[]{:S(2)}) copy-start(bf16[2048,128]{1,0:T(8,128)(2,1)} %wq_hbm.1) | copy-start | bytes 1572868
  1.0 1.0 %copy-start.1 = (bf16[2048,128]{1,0:T(8,128)(2,1)S(1)}, bf16[2048,128]{1,0:T(8,128)(2,1)}, u32[]{:S(2)}) copy-start(bf16[2048,128]{1,0:T(8,128)(2,1)} %wk_hbm.1) | copy-start | bytes 1572868

commit v3 on v2

--- a/solution.py
+++ b/solution.py
@@ -11,7 +11,7 @@
 VALUE_DIM = 128
 ROWS = 160
 PAIR = 2
-LOADS = 2
+LOADS = 4
 MESH = pl.DeviceIdType.MESH
 F32 = jnp.float32
 BF16 = jnp.bfloat16

time: 40.9 us -> 40.2 us (0.983)
  Pallas kernels: 37.3 us -> 36.6 us
    pallas_call x1, Pallas kernels: 37.3 us -> 36.6 us  [per_device(): pl.pallas_call(functools.partial(kernel, n_seq, chunk), out_shape=jax.Sha...]
where the time goes in v3:
time: 40.2 us; the launch traced here: 40 us
  Pallas kernels  36.6 us (91%)
  local copies, waits for them, and re-layouts  3.4 us (8%)
    pallas_call x1, Pallas kernels, per_device(): pl.pallas_call(functools.partial(kernel, n_seq, chunk), out_shape=jax.Sha...  36.6 us
    unnamed x5, local copies, waits for them, and re-layouts  3.4 us

profile of v3, /device:TPU:25, one launch (start us, length us, event | category | flops | bytes accessed | tf_op | source)
XLA Modules:
  0.0 40.0 jit_solution(6743987877843633413)
XLA Ops:
  0.0 0.0 copy-start
  0.0 1.0 %copy-done = bf16[2048,128]{1,0:T(8,128)(2,1)S(1)} copy-done((bf16[2048,128]{1,0:T(8,128)(2,1)S(1)}, bf16[2048,128]{1,0:T(8,128)(2,1)}, u32[]{:S(2)}) %copy-start) | copy-done | bytes 524312
  1.0 0.0 copy-start.1
  1.0 1.0 %copy-done.1 = bf16[2048,128]{1,0:T(8,128)(2,1)S(1)} copy-done((bf16[2048,128]{1,0:T(8,128)(2,1)S(1)}, bf16[2048,128]{1,0:T(8,128)(2,1)}, u32[]{:S(2)}) %copy-start.1) | copy-done | bytes 524312
  2.1 36.6 %shard_map.55 = bf16[1024,1024]{1,0:T(8,128)(2,1)S(1)} custom-call(bf16[1024,2048]{1,0:T(8,128)(2,1)} %tok_hbm.1, bf16[2048,128]{1,0:T(8,128)(2,1)S(1)} %copy-done, bf16[2048,128]{1,0:T(8,128)(2,1)S(1)} %copy-done.1, bf16[2048,1024]{1,0:T(8,128)(2,1)} %wv_hbm.1, bf16[2048,2048]{1,0:T(8,128)(2,1)} %wo_hbm.1), custom_call_target="tpu_custom_call" | custom-call | tf_op jit(solution)/shard_map/pallas_call | solution.py:323
  38.7 1.3 %copy.7 = bf16[1024,1024]{1,0:T(8,128)(2,1)} copy(bf16[1024,1024]{1,0:T(8,128)(2,1)S(1)} %shard_map.55) | data formatting | bytes 4194304
Async XLA Ops:
  0.0 1.0 %copy-start = (bf16[2048,128]{1,0:T(8,128)(2,1)S(1)}, bf16[2048,128]{1,0:T(8,128)(2,1)}, u32[]{:S(2)}) copy-start(bf16[2048,128]{1,0:T(8,128)(2,1)} %wq_hbm.1) | copy-start | bytes 1572868
  1.0 1.0 %copy-start.1 = (bf16[2048,128]{1,0:T(8,128)(2,1)S(1)}, bf16[2048,128]{1,0:T(8,128)(2,1)}, u32[]{:S(2)}) copy-start(bf16[2048,128]{1,0:T(8,128)(2,1)} %wk_hbm.1) | copy-start | bytes 1572868
